TPU v7x, 256 devices: a whole 4x4x8 slice. The times are simulated.
256 devices in a mesh: dp: 64 (over x, z_hi, y), mp: 4 (over z_lo, core).
Axes of the slice: x: 4, y: 4, z: 8 (z_hi: 4, z_lo: 2; z = z_hi * 2 + z_lo), core: 2. Of those that a mesh axis runs over, the one named last changes fastest.
Arguments:
- history_sequences: float32 [512, 512], P('dp'), may hold values from -65 to 65, as said below
- later_steps: float32 [512, 128], P('dp'), may hold values from -65 to 65
- patch_lift_matrix: bfloat16 [32, 1280], P(None, 'dp'), may hold values from -1 to 1
- scaling_factors: bfloat16 [2, 1280], P(None, 'dp'), may hold values from 0.5 to 1.5
- asking_matrix: bfloat16 [1280, 1280], P('dp', 'mp'), may hold values from -0.15625 to 0.15625
- lookup_matrix: bfloat16 [1280, 1280], P('dp', 'mp'), may hold values from -0.15625 to 0.15625
- content_matrix: bfloat16 [1280, 1280], P('dp', 'mp'), may hold values from -0.15625 to 0.15625
- attend_exit_matrix: bfloat16 [1280, 1280], P('mp', 'dp'), may hold values from -0.15625 to 0.15625
- outlook_matrix: bfloat16 [1280, 1280], P('dp', 'mp'), may hold values from -0.15625 to 0.15625
Outputs:
- loss_mean: float32 [], replicated
- embed_grad: float32 [32, 1280], P(None, 'dp')
- gains_grad: float32 [2, 1280], P(None, 'dp')
- query_grad: float32 [1280, 1280], P('dp', 'mp')
- key_grad: float32 [1280, 1280], P('dp', 'mp')
- value_grad: float32 [1280, 1280], P('dp', 'mp')
- output_grad: float32 [1280, 1280], P('mp', 'dp')
- head_weight_gradient: float32 [1280, 1280], P('dp', 'mp')
Inputs may be any that keep to these rules, and one draw needn't show every extreme that they name: `history_sequences`: later_steps continues the history of each series.
All inputs are finite; a program needn't handle non-finite values.
Results may differ from a plain program's by a relative error of at most 0.005.
Values may be sent and summed in bfloat16 or wider, within the bound.
No kernel may reach another device: no remote copies, remote signals or barrier semaphores. Data moves between devices by JAX's collectives and lax.ppermute only.
A program may use at most 64 MiB of HBM per device.

v0:
```python
import math
import jax
import jax.numpy as jnp
from jax import lax
from jax.sharding import Mesh
from jax.sharding import PartitionSpec as P

PATCH = 32
HORIZON_SPAN = 128
PATCHES = 16
LEVEL_CHANNELS = 10
HEAD_DIM = 80
DP = ("dp_0", "dp_1", "dp_2")
MP = ("mp_0", "mp_1")
DP_MP = ("dp_0", "dp_1", "dp_2", "mp_0", "mp_1")
EPS = 1e-06
STAT_EPS = 1e-05
SMOOTHING_RADIUS = 0.05


def gather_turned(arrays, axis, dims):
    turned = [jnp.moveaxis(a, dim, 0) for a, dim in zip(arrays, dims)]
    both = jnp.concatenate([t.reshape(len(t), -1) for t in turned], axis=1)
    out, at, outs = (lax.all_gather(both, axis, axis=0, tiled=True), 0, [])
    for t, dim in zip(turned, dims):
        piece = out[:, at : at + t[0].size].reshape(-1, *t.shape[1:])
        outs.append(jnp.moveaxis(piece, 0, dim))
        at += t[0].size
    return tuple(outs)


def in_one_piece(arrays, axis, dim, along):
    ends, at = ([], 0)
    for a in arrays[:-1]:
        at += a.shape[along]
        ends.append(at)
    both = jnp.concatenate(arrays, axis=along)
    return tuple(jnp.split(lax.all_gather(both, axis, axis=dim, tiled=True), ends, axis=along))


def from_everyone(x, axis):
    length = lax.axis_size(axis)
    return lax.all_to_all(jnp.broadcast_to(x[None], (length, *x.shape)), axis, 0, 0, tiled=True)


def over_copies(x, axis):
    return from_everyone(x, axis).sum(axis=0)


def by_axis(x, axes):
    for axis in axes:
        x = lax.psum(x, axis)
    return x


def taken_together(x, axis):
    return from_everyone(x, axis).astype(jnp.float32).sum(axis=0)


def split_up(x, dim, length):
    before, after = (x.shape[:dim], x.shape[dim + 1 :])
    return jnp.moveaxis(x.reshape(*before, length, -1, *after), dim, 0)


def sum_at_owner(x, axis, dim):
    length = lax.axis_size(axis)
    tiles = lax.all_to_all(split_up(x, dim, length), axis, 0, 0, tiled=True)
    return jnp.sum(tiles.astype(jnp.float32), axis=0)


def sent_together(arrays, axis, dim, along):
    ends, at = ([], 0)
    for a in arrays[:-1]:
        at += a.shape[along]
        ends.append(at)
    both = jnp.concatenate(arrays, axis=along)
    return tuple(jnp.split(sum_at_owner(both, axis, dim), ends, axis=along))


def summed_on_arrival(x, axis, dim):
    tiles = split_up(x, dim, lax.axis_size(axis))
    arrived = lax.all_to_all(tiles, axis, split_axis=0, concat_axis=0, tiled=True)
    return arrived.sum(axis=0)


def sent_together_2(arrays, axis, dim, along):
    both = jnp.concatenate(arrays, axis=along)
    out, at, outs = (summed_on_arrival(both, axis, dim), 0, [])
    for a in arrays:
        outs.append(lax.slice_in_dim(out, at, at + a.shape[along], axis=along))
        at += a.shape[along]
    return tuple(outs)


def rms_forward(residual, gain):
    factor = lax.rsqrt(jnp.mean(residual * residual, axis=1, keepdims=True) + EPS)
    return ((residual * factor * gain[None, :]).astype(jnp.bfloat16), factor)


def rms_backward(residual, factor, gain, upstream):
    weighted = gain[None, :] * upstream
    inner = jnp.mean(weighted * residual, axis=1, keepdims=True)
    back = factor * weighted - residual * factor * factor * factor * inner
    gain_term = jnp.sum(upstream * residual * factor, axis=0)
    return (back, gain_term)


def positions(length, width):
    half = width // 2
    freqs = jnp.exp(-math.log(10000.0) * jnp.arange(half, dtype=jnp.float32) / half)
    angles = jnp.arange(length, dtype=jnp.float32)[:, None] * freqs[None, :]
    return jnp.concatenate([jnp.sin(angles), jnp.cos(angles)], axis=1)


def prepare(history_sequences, later_steps):
    number = history_sequences.shape[0]
    centre = jnp.mean(history_sequences, axis=1, keepdims=True)
    spread = jnp.sqrt(
        jnp.mean((history_sequences - centre) * (history_sequences - centre), axis=1, keepdims=True)
        + STAT_EPS
    )
    normed = (history_sequences - centre) / spread
    ahead = (later_steps - centre) / spread
    joined = jnp.concatenate([normed, ahead], axis=1).reshape(number, -1, PATCH)
    reach = later_steps.shape[1] // PATCH
    future_values = jnp.concatenate(
        [joined[:, offset + 1 : offset + 1 + PATCHES] for offset in range(reach)], axis=2
    )
    future_values = future_values.reshape(number * PATCHES, reach * PATCH)
    patches = normed.reshape(number * PATCHES, PATCH).astype(jnp.bfloat16)
    return (patches, future_values)


def attention_forward(queries, keys, values, number):
    layout = (number, PATCHES, -1, HEAD_DIM)
    query_blocks = queries.reshape(layout)
    key_blocks = keys.reshape(layout)
    value_blocks = values.reshape(layout)
    scale = 1.0 / math.sqrt(HEAD_DIM)
    scores = (
        jnp.einsum("sihd,sjhd->shij", query_blocks, key_blocks, preferred_element_type=jnp.float32)
        * scale
    )
    place = jnp.arange(PATCHES)
    causal = place[:, None] >= place[None, :]
    raised = jnp.where(causal, jnp.exp(scores), 0.0)
    probs = raised / jnp.sum(raised, axis=3, keepdims=True)
    probs_low = probs.astype(jnp.bfloat16)
    context = jnp.einsum(
        "shij,sjhd->sihd", probs_low, value_blocks, preferred_element_type=jnp.float32
    )
    context = context.astype(jnp.bfloat16).reshape(number * PATCHES, -1)
    return (context, probs, probs_low)


def attention_backward(context_grad, queries, keys, values, probs, probs_low, number):
    layout = (number, PATCHES, -1, HEAD_DIM)
    query_blocks = queries.reshape(layout)
    key_blocks = keys.reshape(layout)
    value_blocks = values.reshape(layout)
    grad_blocks = context_grad.reshape(layout)
    scale = 1.0 / math.sqrt(HEAD_DIM)
    prob_grad = jnp.einsum(
        "sihd,sjhd->shij", grad_blocks, value_blocks, preferred_element_type=jnp.float32
    )
    value_back = jnp.einsum(
        "shij,sihd->sjhd", probs_low, grad_blocks, preferred_element_type=jnp.float32
    ).astype(jnp.bfloat16)
    centred = prob_grad - jnp.sum(probs * prob_grad, axis=3, keepdims=True)
    score_grad = (probs * centred * scale).astype(jnp.bfloat16)
    query_back = jnp.einsum(
        "shij,sjhd->sihd", score_grad, key_blocks, preferred_element_type=jnp.float32
    ).astype(jnp.bfloat16)
    key_back = jnp.einsum(
        "shij,sihd->sjhd", score_grad, query_blocks, preferred_element_type=jnp.float32
    ).astype(jnp.bfloat16)
    flat = (number * PATCHES, -1)
    return (query_back.reshape(flat), key_back.reshape(flat), value_back.reshape(flat))


def pinball_terms(estimate_entries, actual_entries):
    batch_example_tally = estimate_entries.shape[0]
    horizon_error = actual_entries[:, :, None] - estimate_entries.reshape(
        batch_example_tally, -1, LEVEL_CHANNELS
    )
    cumulative_share = jnp.arange(LEVEL_CHANNELS, dtype=jnp.float32) / LEVEL_CHANNELS
    mean_indicator = jnp.arange(LEVEL_CHANNELS) == 0
    lopsided_errors = jnp.where(
        mean_indicator,
        horizon_error * horizon_error,
        cumulative_share * horizon_error
        + SMOOTHING_RADIUS * jax.nn.softplus(-horizon_error / SMOOTHING_RADIUS),
    )
    skew_coefficient = (
        jnp.where(
            mean_indicator,
            -2.0 * horizon_error,
            jax.nn.sigmoid(-horizon_error / SMOOTHING_RADIUS) - cumulative_share,
        )
        / HORIZON_SPAN
    )
    return (
        jnp.sum(lopsided_errors) / HORIZON_SPAN,
        skew_coefficient.reshape(batch_example_tally, -1).astype(jnp.bfloat16),
    )


def multiplied_rows(left, right):

    def term(start, count):
        return jnp.dot(left, right, preferred_element_type=jnp.float32)

    return term


def per_device(
    history_sequences,
    later_steps,
    patch_lift_matrix,
    scaling_factors,
    asking_matrix,
    lookup_matrix,
    content_matrix,
    attend_exit_matrix,
    outlook_matrix,
):
    number = history_sequences.shape[0]
    rows_all = number * PATCHES
    patches, future_values = prepare(history_sequences, later_steps)
    embed_full, gains_full = gather_turned((patch_lift_matrix, scaling_factors), DP, (1, 1))
    gains = gains_full.astype(jnp.float32)
    query_full, key_full, value_full, outlook_collected = in_one_piece(
        (asking_matrix, lookup_matrix, content_matrix, outlook_matrix), DP, 0, 1
    )
    output_full = lax.all_gather(attend_exit_matrix, DP, axis=1, tiled=True)
    residual_zero = jnp.dot(patches, embed_full, preferred_element_type=jnp.float32) + jnp.tile(
        positions(PATCHES, embed_full.shape[1]), (number, 1)
    )
    normed_attn, factor_attn = rms_forward(residual_zero, gains[0])
    queries = jnp.dot(normed_attn, query_full, preferred_element_type=jnp.float32).astype(
        jnp.bfloat16
    )
    keys = jnp.dot(normed_attn, key_full, preferred_element_type=jnp.float32).astype(jnp.bfloat16)
    values = jnp.dot(normed_attn, value_full, preferred_element_type=jnp.float32).astype(
        jnp.bfloat16
    )
    context, probs, probs_low = attention_forward(queries, keys, values, number)
    attn_term = multiplied_rows(context, output_full)
    residual_one = residual_zero + over_copies(attn_term(0, rows_all), MP)
    normed_head, factor_head = rms_forward(residual_one, gains[1])
    estimate_entries = jnp.dot(normed_head, outlook_collected, preferred_element_type=jnp.float32)
    device_portion = estimate_entries.shape[1] // LEVEL_CHANNELS
    actual_entries = lax.dynamic_slice_in_dim(
        future_values, lax.axis_index(MP) * device_portion, device_portion, 1
    )
    device_loss, estimate_derivative = pinball_terms(estimate_entries, actual_entries)
    total_loss_value = by_axis(device_loss, DP_MP)
    loss_mean = total_loss_value / (number * PATCHES * lax.axis_size(DP))
    head_weight_gradient = jnp.dot(
        normed_head.T, estimate_derivative, preferred_element_type=jnp.float32
    )
    head_contribution = multiplied_rows(estimate_derivative, outlook_collected.T)
    head_reverse = taken_together(head_contribution(0, rows_all).astype(jnp.bfloat16), MP).astype(
        jnp.float32
    )
    residual_one_grad, gain_one = rms_backward(residual_one, factor_head, gains[1], head_reverse)
    attn_low = residual_one_grad.astype(jnp.bfloat16)
    output_grad = jnp.dot(context.T, attn_low, preferred_element_type=jnp.float32)
    context_grad = jnp.dot(attn_low, output_full.T, preferred_element_type=jnp.float32).astype(
        jnp.bfloat16
    )
    query_back, key_back, value_back = attention_backward(
        context_grad, queries, keys, values, probs, probs_low, number
    )
    query_grad = jnp.dot(normed_attn.T, query_back, preferred_element_type=jnp.float32)
    key_grad = jnp.dot(normed_attn.T, key_back, preferred_element_type=jnp.float32)
    value_grad = jnp.dot(normed_attn.T, value_back, preferred_element_type=jnp.float32)
    total = jnp.dot(query_back, query_full.T, preferred_element_type=jnp.float32)
    total = total + jnp.dot(key_back, key_full.T, preferred_element_type=jnp.float32)
    attn_back = taken_together(
        (total + jnp.dot(value_back, value_full.T, preferred_element_type=jnp.float32)).astype(
            jnp.bfloat16
        ),
        MP,
    ).astype(jnp.float32)
    norm_back_zero, gain_zero = rms_backward(residual_zero, factor_attn, gains[0], attn_back)
    residual_zero_grad = residual_one_grad + norm_back_zero
    embed_grad = jnp.dot(
        patches.T, residual_zero_grad.astype(jnp.bfloat16), preferred_element_type=jnp.float32
    )
    gains_grad = jnp.stack([gain_zero, gain_one], axis=0)
    query_grad, key_grad, value_grad, head_weight_gradient = sent_together(
        (
            query_grad.astype(jnp.bfloat16),
            key_grad.astype(jnp.bfloat16),
            value_grad.astype(jnp.bfloat16),
            head_weight_gradient.astype(jnp.bfloat16),
        ),
        DP,
        0,
        1,
    )
    output_grad = sum_at_owner(output_grad.astype(jnp.bfloat16), DP, 1)
    embed_grad, gains_grad = sent_together_2((embed_grad, gains_grad), DP, 1, 0)
    return (
        loss_mean,
        embed_grad,
        gains_grad,
        query_grad,
        key_grad,
        value_grad,
        output_grad,
        head_weight_gradient,
    )


def solution(mesh):
    split = Mesh(mesh.devices.reshape(4, 4, 4, 2, 2), ("dp_0", "dp_1", "dp_2", "mp_0", "mp_1"))
    placed = (
        P(DP, None),
        P(DP, None),
        P(None, DP),
        P(None, DP),
        P(DP, MP),
        P(DP, MP),
        P(DP, MP),
        P(MP, DP),
        P(DP, MP),
    )
    return jax.shard_map(
        per_device,
        mesh=split,
        in_specs=placed,
        out_specs=(
            P(),
            P(None, DP),
            P(None, DP),
            P(DP, MP),
            P(DP, MP),
            P(DP, MP),
            P(MP, DP),
            P(DP, MP),
        ),
        check_vma=False,
    )
```

profile of v0, /device:TPU:1, one launch (start us, length us, event | category | flops | bytes accessed | tf_op | source)
XLA Modules:
  0.0 718.7 jit_solution(1902449885133331667)
XLA Ops:
  7.2 1.5 concatenate.30
  12.9 172.1 %all-gather = bf16[64,20,34]{2,1,0:T(8,128)(2,1)S(1)} all-gather(bf16[1,20,34]{2,1,0:T(8,128)(2,1)S(1)} %maximum_bitcast_fusion.1), channel_id=1, replica_groups=mesh['dp_0'=4,'dp_1'=4,'dp_2'=4,'mp_0'=2,'mp_1'=2] {'dp_0','dp_1','dp_2'}, dimensions={0}, use_global_device_ids=true | all-gather | bytes 88400 | tf_op jit(solution)/shard_map/all_gather | solution.py:24
  185.5 164.7 %all-gather.2 = bf16[64,20,320]{2,1,0:T(8,128)(2,1)S(1)} all-gather(bf16[1,20,320]{2,1,0:T(8,128)(2,1)} %bitcast.63), channel_id=1, replica_groups=mesh['dp_0'=4,'dp_1'=4,'dp_2'=4,'mp_0'=2,'mp_1'=2] {'dp_0','dp_1','dp_2'}, dimensions={0}, use_global_device_ids=true | all-gather | bytes 832000 | tf_op jit(solution)/shard_map/all_gather | solution.py:235
  351.5 6.2 reshape.143
  357.7 1.7 convolution_convert_fusion.13
  359.4 2.3 convolution_convert_fusion.11
  361.7 1.7 convolution_convert_fusion.12
  365.4 1.7 broadcast_in_dim.61
  367.1 57.9 %all-to-all-start = ((f32[4,128,1280]{2,1,0:T(8,128)}), f32[4,128,1280]{2,1,0:T(8,128)S(1)}, u32[]{:S(2)}, u32[]{:S(2)}) async-start(f32[4,128,1280]{2,1,0:T(8,128)} %broadcast_in_dim.61), calls=%async_computation | async-start | bytes 5242880 | tf_op jit(solution)/shard_map/all_to_all | solution.py:43
  428.8 26.1 %all-to-all-done = f32[4,128,1280]{2,1,0:T(8,128)S(1)} async-done(((f32[4,128,1280]{2,1,0:T(8,128)}), f32[4,128,1280]{2,1,0:T(8,128)S(1)}, u32[]{:S(2)}, u32[]{:S(2)}) %all-to-all-start) | async-done | bytes 2621472 | tf_op jit(solution)/shard_map/all_to_all | solution.py:43
  456.0 1.2 multiply_reduce_fusion.4
  457.3 2.9 fusion.32
  460.2 2.1 convolution_convert_fusion.5
  462.2 1.2 broadcast_in_dim.62
  463.4 5.5 all-to-all-start.1
  469.7 15.6 %all-to-all-done.1 = bf16[4,128,1280]{2,1,0:T(8,128)(2,1)} async-done(((bf16[4,128,1280]{2,1,0:T(8,128)(2,1)}), bf16[4,128,1280]{2,1,0:T(8,128)(2,1)}, u32[]{:S(2)}, u32[]{:S(2)}) %all-to-all-start.1) | async-done | bytes 1310752 | tf_op jit(solution)/shard_map/all_to_all | solution.py:43
  485.3 1.6 convert_reduce_fusion.2
  488.4 1.3 fusion.9
  489.7 1.3 fusion.10
  490.9 1.2 fusion.11
  492.4 1.7 fusion.16
  494.5 1.9 convolution_add_fusion.1
  496.4 1.6 fusion.1
  499.1 4.7 all-to-all-start.2
  503.8 2.3 convolution_convert_fusion
  506.3 2.2 convolution_convert_fusion.1
  508.5 2.2 copy.121
  510.7 2.2 reshape.139
  512.9 1.3 convolution_convert_fusion.2
  514.3 1.3 convolution_convert_fusion.3
  515.6 4.5 all-to-all-done.2
  520.1 5.5 all-to-all-start.5
  525.6 1.3 convolution_convert_fusion.4
  528.5 1.2 copy.118
  529.7 2.4 reshape.150
  532.1 25.7 %all-to-all-done.5 = bf16[64,320,20]{1,2,0:T(8,128)(2,1)} async-done(((bf16[64,320,20]{1,2,0:T(8,128)(2,1)}), bf16[64,320,20]{1,2,0:T(8,128)(2,1)}, u32[]{:S(2)}, u32[]{:S(2)}) %all-to-all-start.5) | async-done | bytes 819232 | tf_op jit(solution)/shard_map/all_to_all | solution.py:67
  557.8 7.1 all-to-all-start.3
  565.0 3.0 pad_maximum_fusion
  568.0 5.7 copy.120
  573.7 6.1 reshape.138
  579.7 12.4 %all-to-all-start.4 = ((bf16[64,20,1280]{2,1,0:T(8,128)(2,1)}), bf16[64,20,1280]{2,1,0:T(8,128)(2,1)}, u32[]{:S(2)}, u32[]{:S(2)}) async-start(bf16[64,20,1280]{2,1,0:T(8,128)(2,1)} %reshape.138), calls=%async_computation.4 | async-start | bytes 7864320 | tf_op jit(solution)/shard_map/all_to_all | solution.py:67
  592.8 16.2 %psum.35 = f32[]{:T(128)} all-reduce(f32[]{:T(128)S(6)} %div.89), channel_id=1, replica_groups=mesh['dp_0'=4,'dp_1'=4,'dp_2'=4,'mp_0'=2,'mp_1'=2] {'dp_0'}, use_global_device_ids=true, to_apply=%region_7.8 | all-reduce | flops 1 | bytes 8 | tf_op jit(solution)/shard_map/psum | solution.py:52
  609.0 68.8 %psum.36 = f32[]{:T(128)} all-reduce(f32[]{:T(128)} %psum.35), channel_id=1, replica_groups=mesh['dp_0'=4,'dp_1'=4,'dp_2'=4,'mp_0'=2,'mp_1'=2] {'dp_1'}, use_global_device_ids=true, to_apply=%region_8.9 | all-reduce | flops 1 | bytes 8 | tf_op jit(solution)/shard_map/psum | solution.py:52
  677.8 12.2 %psum.37 = f32[]{:T(128)} all-reduce(f32[]{:T(128)} %psum.36), channel_id=1, replica_groups=mesh['dp_0'=4,'dp_1'=4,'dp_2'=4,'mp_0'=2,'mp_1'=2] {'dp_2'}, use_global_device_ids=true, to_apply=%region_9.10 | all-reduce | flops 1 | bytes 8 | tf_op jit(solution)/shard_map/psum | solution.py:52
  690.0 4.4 psum.38
  694.4 7.3 %psum.39 = f32[]{:T(128)} all-reduce(f32[]{:T(128)} %psum.38), channel_id=1, replica_groups=mesh['dp_0'=4,'dp_1'=4,'dp_2'=4,'mp_0'=2,'mp_1'=2] {'mp_1'}, use_global_device_ids=true, to_apply=%region_11.12 | all-reduce | flops 1 | bytes 8 | tf_op jit(solution)/shard_map/psum | solution.py:52
  702.4 2.1 convert_reduce_fusion.3
  707.2 2.8 convert_reduce_fusion
  (142 shorter events, 21.7 us)
Async XLA Ops:
  7.2 344.3 %all-gather.5.cloned.1.call-start = ((), (), s32[]{:S(2)}) async-start(), calls=%async_computation.6 | async-start | bytes 3993600 | tf_op jit(solution)/shard_map/all_gather | solution.py:38
  11.4 339.6 %copy-start.11 = (bf16[128,32]{1,0:T(8,128)(2,1)}, bf16[128,32]{1,0:T(8,128)(2,1)S(1)}, u32[]{:S(2)}) copy-start(bf16[128,32]{1,0:T(8,128)(2,1)S(1)} %convert_element_type.104) | copy-start | bytes 24580
  350.6 14.3 %copy-start = (bf16[1280,320]{1,0:T(8,128)(2,1)}, bf16[1280,320]{1,0:T(8,128)(2,1)S(1)}, u32[]{:S(2)}) copy-start(bf16[1280,320]{1,0:T(8,128)(2,1)S(1)} %reshape.145) | copy-start | bytes 2457604
  351.3 6.4 copy-start.21
  351.4 10.3 %copy-start.2 = (bf16[128,1280]{1,0:T(8,128)(2,1)}, bf16[128,1280]{1,0:T(8,128)(2,1)S(1)}, u32[]{:S(2)}) copy-start(bf16[128,1280]{1,0:T(8,128)(2,1)S(1)} %multiply_convert_fusion.1) | copy-start | bytes 983044
  363.7 0.8 copy-start.9
  363.9 3.1 copy-start.15
  364.2 2.9 copy-start.17
  364.5 2.6 copy-start.25
  364.9 2.2 copy-start.6
  367.1 59.2 %copy-start.23 = (f32[8,128]{1,0:T(8,128)S(1)}, f32[8,128]{1,0:T(8,128)}, u32[]{:S(2)}) copy-start(f32[8,128]{1,0:T(8,128)} %param.10) | copy-start | bytes 12292
  367.1 87.9 %all-to-all-start = ((f32[4,128,1280]{2,1,0:T(8,128)}), f32[4,128,1280]{2,1,0:T(8,128)S(1)}, u32[]{:S(2)}, u32[]{:S(2)}) async-start(f32[4,128,1280]{2,1,0:T(8,128)} %broadcast_in_dim.61), calls=%async_computation | async-start | bytes 5242880 | tf_op jit(solution)/shard_map/all_to_all | solution.py:43
  428.8 28.4 %copy-start.13 = (f32[128,320]{0,1:T(8,128)S(1)}, f32[128,320]{0,1:T(8,128)}, u32[]{:S(2)}) copy-start(f32[128,320]{0,1:T(8,128)} %sub.62) | copy-start | bytes 491524
  428.8 28.4 %copy-start.20 = (f32[320]{0:T(512)S(1)}, f32[320]{0:T(512)}, u32[]{:S(2)}) copy-start(f32[320]{0:T(512)} %mul.236) | copy-start | bytes 3844
  428.8 28.4 %copy-start.24 = (pred[320]{0:T(512)(128)(4,1)S(1)}, pred[320]{0:T(512)(128)(4,1)}, u32[]{:S(2)}) copy-start(pred[320]{0:T(512)(128)(4,1)} %broadcast_in_dim.30) | copy-start | bytes 964
  460.2 3.2 copy-start.14
  460.2 8.8 %copy-start.26 = (f32[8,4,16,16]{2,3,1,0:T(8,128)S(1)}, f32[8,4,16,16]{2,3,1,0:T(8,128)}, u32[]{:S(2)}) copy-start(f32[8,4,16,16]{2,3,1,0:T(8,128)} %copy-done.25) | copy-start | bytes 98308
  463.4 21.9 %all-to-all-start.1 = ((bf16[4,128,1280]{2,1,0:T(8,128)(2,1)}), bf16[4,128,1280]{2,1,0:T(8,128)(2,1)}, u32[]{:S(2)}, u32[]{:S(2)}) async-start(bf16[4,128,1280]{2,1,0:T(8,128)(2,1)} %broadcast_in_dim.62), calls=%async_computation.1 | async-start | bytes 2621440 | tf_op jit(solution)/shard_map/all_to_all | solution.py:43
  468.9 18.4 %copy-start.1 = (bf16[1280,320]{1,0:T(8,128)(2,1)S(1)}, bf16[1280,320]{1,0:T(8,128)(2,1)}, u32[]{:S(2)}) copy-start(bf16[1280,320]{1,0:T(8,128)(2,1)} %copy-done) | copy-start | bytes 2457604
  469.7 18.4 %copy-start.10 = (bf16[8,16,4,80]{3,2,1,0:T(4,128)(2,1)S(1)}, bf16[8,16,4,80]{3,2,1,0:T(4,128)(2,1)}, u32[]{:S(2)}) copy-start(bf16[8,16,4,80]{3,2,1,0:T(4,128)(2,1)} %copy-done.9) | copy-start | bytes 245764
  486.9 1.5 copy-start.16
  486.9 2.7 copy-start.18
  492.4 5.6 copy-start.7
  499.1 20.9 %all-to-all-start.2 = ((bf16[4,128,1280]{2,1,0:T(8,128)(2,1)}), bf16[4,128,1280]{2,1,0:T(8,128)(2,1)S(1)}, u32[]{:S(2)}, u32[]{:S(2)}) async-start(bf16[4,128,1280]{2,1,0:T(8,128)(2,1)} %broadcast_in_dim.63), calls=%async_computation.2 | async-start | bytes 2621440 | tf_op jit(solution)/shard_map/all_to_all | solution.py:43
  506.1 6.9 copy-start.3
  510.7 14.8 %copy-start.8 = (bf16[128,320]{1,0:T(8,128)(2,1)S(1)}, bf16[128,320]{1,0:T(8,128)(2,1)}, u32[]{:S(2)}) copy-start(bf16[128,320]{1,0:T(8,128)(2,1)} %copy-done.7) | copy-start | bytes 245764
  514.3 12.8 %copy-start.22 = (f32[128]{0:T(128)S(1)}, f32[128]{0:T(128)}, u32[]{:S(2)}) copy-start(f32[128]{0:T(128)} %copy-done.21) | copy-start | bytes 1540
  520.1 37.8 %all-to-all-start.5 = ((bf16[64,320,20]{1,2,0:T(8,128)(2,1)}), bf16[64,320,20]{1,2,0:T(8,128)(2,1)}, u32[]{:S(2)}, u32[]{:S(2)}) async-start(bf16[64,320,20]{1,2,0:T(8,128)(2,1)} %bitcast.55), calls=%async_computation.5 | async-start | bytes 2359296 | tf_op jit(solution)/shard_map/all_to_all | solution.py:67
  526.9 1.1 copy-start.12
  527.5 37.5 %copy-start.4 = (bf16[1280,320]{0,1:T(8,128)(2,1)S(1)}, bf16[1280,320]{0,1:T(8,128)(2,1)}, u32[]{:S(2)}) copy-start(bf16[1280,320]{0,1:T(8,128)(2,1)} %convolution_convert_fusion.2) | copy-start | bytes 2457604
  527.7 37.3 %copy-start.5 = (bf16[1280,320]{0,1:T(8,128)(2,1)S(1)}, bf16[1280,320]{0,1:T(8,128)(2,1)}, u32[]{:S(2)}) copy-start(bf16[1280,320]{0,1:T(8,128)(2,1)} %convolution_convert_fusion.3) | copy-start | bytes 2457604
  557.8 21.9 %all-to-all-start.3 = ((f32[64,1,680]{2,1,0:T(1,128)}), f32[64,1,680]{2,1,0:T(1,128)S(1)}, u32[]{:S(2)}, u32[]{:S(2)}) async-start(f32[64,1,680]{2,1,0:T(1,128)} %reshape.150), calls=%async_computation.3 | async-start | bytes 393216 | tf_op jit(solution)/shard_map/all_to_all | solution.py:82
  579.7 127.5 %all-to-all-start.4 = ((bf16[64,20,1280]{2,1,0:T(8,128)(2,1)}), bf16[64,20,1280]{2,1,0:T(8,128)(2,1)}, u32[]{:S(2)}, u32[]{:S(2)}) async-start(bf16[64,20,1280]{2,1,0:T(8,128)(2,1)} %reshape.138), calls=%async_computation.4 | async-start | bytes 7864320 | tf_op jit(solution)/shard_map/all_to_all | solution.py:67
  706.5 4.2 copy-start.19
Sparse Core Ops, SparseCore 0:
  11.2 90.6 all-gather.4
where the time goes:
time: 721 us; the launch traced here: 719 us
  blocking collectives  446 us (62%)
  starting transfers between devices  93.1 us (13%)
  waiting for transfers between devices  72 us (10%)
  local copies, waits for them, and re-layouts  41.5 us (6%)
  matrix products  30.4 us (4%)
  other arithmetic  18.8 us (3%)
  between operations  17.2 us (2%)
    all_gather x1, blocking collectives, gather_turned(): out, at, outs = (lax.all_gather(both, axis, axis=0, tiled=True), 0, [])  172 us
    all_gather x1, blocking collectives, per_device(): output_full = lax.all_gather(attend_exit_matrix, DP, axis=1, tiled=True)  165 us
    psum x5, blocking collectives, by_axis(): x = lax.psum(x, axis)  109 us
    all_to_all x3, starting transfers between devices, from_everyone(): lax.all_to_all(jnp.broadcast_to(x[None], (length, *x.shape)), axis, 0, 0,...  68 us
    all_to_all x3, waiting for transfers between devices, from_everyone(): lax.all_to_all(jnp.broadcast_to(x[None], (length, *x.shape)), axis, 0, 0,...  46.2 us
    all_to_all x2, waiting for transfers between devices, sum_at_owner(): tiles = lax.all_to_all(split_up(x, dim, length), axis, 0, 0, tiled=True)  25.7 us
    all_to_all x2, starting transfers between devices, sum_at_owner(): tiles = lax.all_to_all(split_up(x, dim, length), axis, 0, 0, tiled=True)  17.9 us
  transfers between devices with their start and end apart: 7, of which 4 were waited for; matrix products, arithmetic and copies ran while one was open for 7% of the time, Pallas kernels for 0%

commit v1 on v0

--- a/solution.py
+++ b/solution.py
@@ -232,7 +232,10 @@
     query_full, key_full, value_full, outlook_collected = in_one_piece(
         (asking_matrix, lookup_matrix, content_matrix, outlook_matrix), DP, 0, 1
     )
-    output_full = lax.all_gather(attend_exit_matrix, DP, axis=1, tiled=True)
+    size = lax.axis_size(DP)
+    blocks = jnp.stack([attend_exit_matrix for _ in range(size)])
+    blocks = lax.all_to_all(blocks, DP, split_axis=0, concat_axis=0)
+    output_full = jnp.concatenate(blocks, axis=1)
     residual_zero = jnp.dot(patches, embed_full, preferred_element_type=jnp.float32) + jnp.tile(
         positions(PATCHES, embed_full.shape[1]), (number, 1)
     )

time: 721 us -> 550 us (0.76)
  blocking collectives: 446 us -> 294 us
  starting transfers between devices: 93.1 us -> 77.5 us
    all_gather x1 -> x0, blocking collectives: 165 us -> none  [per_device(): output_full = lax.all_gather(attend_exit_matrix, DP, axis=1, tiled=True)]
    all_to_all x3, starting transfers between devices: 68 us -> 40.4 us  [from_everyone(): lax.all_to_all(jnp.broadcast_to(x[None], (length, *x.shape)), axis, 0, 0,...]
    all_to_all x0 -> x1, starting transfers between devices: none -> 15.1 us  [per_device(): blocks = lax.all_to_all(blocks, DP, split_axis=0, concat_axis=0)]
    all_gather x1, blocking collectives: 172 us -> 185 us  [gather_turned(): out, at, outs = (lax.all_gather(both, axis, axis=0, tiled=True), 0, [])]
  transfers between devices with their start and end apart: 7 -> 8, of which waited for: 4 -> 5; matrix products, arithmetic and copies ran while one was open for 7% -> 8% of each run, Pallas kernels for 0% -> 0%
where the time goes in v1:
time: 550 us; the launch traced here: 549 us
  blocking collectives  294 us (53%)
  starting transfers between devices  77.5 us (14%)
  waiting for transfers between devices  75.3 us (14%)
  local copies, waits for them, and re-layouts  37.9 us (7%)
  matrix products  30.4 us (6%)
  between operations  17.3 us (3%)
  other arithmetic  15.8 us (3%)
    all_gather x1, blocking collectives, gather_turned(): out, at, outs = (lax.all_gather(both, axis, axis=0, tiled=True), 0, [])  185 us
    psum x5, blocking collectives, by_axis(): x = lax.psum(x, axis)  109 us
    all_to_all x3, waiting for transfers between devices, from_everyone(): lax.all_to_all(jnp.broadcast_to(x[None], (length, *x.shape)), axis, 0, 0,...  46.5 us
    all_to_all x3, starting transfers between devices, from_everyone(): lax.all_to_all(jnp.broadcast_to(x[None], (length, *x.shape)), axis, 0, 0,...  40.4 us
    all_to_all x2, waiting for transfers between devices, sum_at_owner(): tiles = lax.all_to_all(split_up(x, dim, length), axis, 0, 0, tiled=True)  25.7 us
    all_to_all x1, starting transfers between devices, per_device(): blocks = lax.all_to_all(blocks, DP, split_axis=0, concat_axis=0)  15.1 us
    all_to_all x2, starting transfers between devices, sum_at_owner(): tiles = lax.all_to_all(split_up(x, dim, length), axis, 0, 0, tiled=True)  14.9 us
  transfers between devices with their start and end apart: 8, of which 5 were waited for; matrix products, arithmetic and copies ran while one was open for 8% of the time, Pallas kernels for 0%

profile of v1, /device:TPU:1, one launch (start us, length us, event | category | flops | bytes accessed | tf_op | source)
XLA Modules:
  0.0 548.6 jit_solution(373888978994468057)
XLA Ops:
  7.2 1.5 concatenate.30
  8.8 1.9 stack.2
  10.6 15.1 %all-to-all-start = ((bf16[64,320,20]{1,2,0:T(8,128)(2,1)}), bf16[64,320,20]{1,2,0:T(8,128)(2,1)S(1)}, u32[]{:S(2)}, u32[]{:S(2)}) async-start(bf16[64,320,20]{1,2,0:T(8,128)(2,1)} %stack.2), calls=%async_computation | async-start | bytes 2359296 | tf_op jit(solution)/shard_map/all_to_all | solution.py:237
  26.5 185.4 %all-gather = bf16[64,20,34]{2,1,0:T(8,128)(2,1)S(1)} all-gather(bf16[1,20,34]{2,1,0:T(8,128)(2,1)S(1)} %maximum_bitcast_fusion.1), channel_id=1, replica_groups=mesh['dp_0'=4,'dp_1'=4,'dp_2'=4,'mp_0'=2,'mp_1'=2] {'dp_0','dp_1','dp_2'}, dimensions={0}, use_global_device_ids=true | all-gather | bytes 88400 | tf_op jit(solution)/shard_map/all_gather | solution.py:24
  213.7 6.4 %reshape.153 = bf16[1280,1280]{1,0:T(8,128)(2,1)} reshape(bf16[64,20,1280]{2,1,0:T(8,128)(2,1)} %all-gather.4.cloned.1.call-done) | data formatting | bytes 6553600
  220.1 1.7 convolution_convert_fusion.13
  221.8 2.3 convolution_convert_fusion.11
  224.2 1.7 convolution_convert_fusion.12
  227.8 1.7 broadcast_in_dim.61
  229.5 30.7 %all-to-all-start.1 = ((f32[4,128,1280]{2,1,0:T(8,128)}), f32[4,128,1280]{2,1,0:T(8,128)S(1)}, u32[]{:S(2)}, u32[]{:S(2)}) async-start(f32[4,128,1280]{2,1,0:T(8,128)} %broadcast_in_dim.61), calls=%async_computation.1 | async-start | bytes 5242880 | tf_op jit(solution)/shard_map/all_to_all | solution.py:43
  264.1 26.4 %all-to-all-done.1 = f32[4,128,1280]{2,1,0:T(8,128)S(1)} async-done(((f32[4,128,1280]{2,1,0:T(8,128)}), f32[4,128,1280]{2,1,0:T(8,128)S(1)}, u32[]{:S(2)}, u32[]{:S(2)}) %all-to-all-start.1) | async-done | bytes 2621472 | tf_op jit(solution)/shard_map/all_to_all | solution.py:43
  291.6 1.2 multiply_reduce_fusion.4
  292.8 2.9 fusion.32
  295.8 2.1 convolution_convert_fusion.5
  299.0 5.2 all-to-all-start.2
  305.0 15.6 %all-to-all-done.2 = bf16[4,128,1280]{2,1,0:T(8,128)(2,1)} async-done(((bf16[4,128,1280]{2,1,0:T(8,128)(2,1)}), bf16[4,128,1280]{2,1,0:T(8,128)(2,1)}, u32[]{:S(2)}, u32[]{:S(2)}) %all-to-all-start.2) | async-done | bytes 1310752 | tf_op jit(solution)/shard_map/all_to_all | solution.py:43
  320.6 1.6 convert_reduce_fusion.2
  323.6 1.3 fusion.9
  324.9 1.3 fusion.10
  326.2 1.2 fusion.11
  327.7 1.7 fusion.16
  329.7 1.9 convolution_add_fusion.1
  331.6 1.6 fusion.1
  334.4 4.5 all-to-all-start.3
  338.9 2.3 convolution_convert_fusion
  341.3 2.2 convolution_convert_fusion.1
  343.6 2.2 copy.122
  345.8 2.2 reshape.149
  348.0 1.3 convolution_convert_fusion.2
  349.3 1.3 convolution_convert_fusion.3
  350.7 4.5 all-to-all-done.3
  355.2 5.5 %all-to-all-start.6 = ((bf16[64,320,20]{1,2,0:T(8,128)(2,1)}), bf16[64,320,20]{1,2,0:T(8,128)(2,1)}, u32[]{:S(2)}, u32[]{:S(2)}) async-start(bf16[64,320,20]{1,2,0:T(8,128)(2,1)} %bitcast.56), calls=%async_computation.6 | async-start | bytes 2359296 | tf_op jit(solution)/shard_map/all_to_all | solution.py:67
  360.7 1.3 convolution_convert_fusion.4
  364.8 2.4 reshape.158
  367.2 25.7 %all-to-all-done.6 = bf16[64,320,20]{1,2,0:T(8,128)(2,1)} async-done(((bf16[64,320,20]{1,2,0:T(8,128)(2,1)}), bf16[64,320,20]{1,2,0:T(8,128)(2,1)}, u32[]{:S(2)}, u32[]{:S(2)}) %all-to-all-start.6) | async-done | bytes 819232 | tf_op jit(solution)/shard_map/all_to_all | solution.py:67
  392.9 7.1 %all-to-all-start.4 = ((f32[64,1,680]{2,1,0:T(1,128)}), f32[64,1,680]{2,1,0:T(1,128)S(1)}, u32[]{:S(2)}, u32[]{:S(2)}) async-start(f32[64,1,680]{2,1,0:T(1,128)} %reshape.158), calls=%async_computation.4 | async-start | bytes 393216 | tf_op jit(solution)/shard_map/all_to_all | solution.py:82
  400.1 2.9 pad_maximum_fusion
  402.9 4.0 copy.121
  407.0 2.6 reshape.148
  409.5 3.0 all-to-all-done.4
  412.5 9.4 %all-to-all-start.5 = ((bf16[64,20,1280]{2,1,0:T(8,128)(2,1)}), bf16[64,20,1280]{2,1,0:T(8,128)(2,1)}, u32[]{:S(2)}, u32[]{:S(2)}) async-start(bf16[64,20,1280]{2,1,0:T(8,128)(2,1)} %reshape.148), calls=%async_computation.5 | async-start | bytes 7864320 | tf_op jit(solution)/shard_map/all_to_all | solution.py:67
  422.6 16.2 %psum.35 = f32[]{:T(128)} all-reduce(f32[]{:T(128)S(6)} %div.89), channel_id=1, replica_groups=mesh['dp_0'=4,'dp_1'=4,'dp_2'=4,'mp_0'=2,'mp_1'=2] {'dp_0'}, use_global_device_ids=true, to_apply=%region_7.8 | all-reduce | flops 1 | bytes 8 | tf_op jit(solution)/shard_map/psum | solution.py:52
  438.8 68.8 %psum.36 = f32[]{:T(128)} all-reduce(f32[]{:T(128)} %psum.35), channel_id=1, replica_groups=mesh['dp_0'=4,'dp_1'=4,'dp_2'=4,'mp_0'=2,'mp_1'=2] {'dp_1'}, use_global_device_ids=true, to_apply=%region_8.9 | all-reduce | flops 1 | bytes 8 | tf_op jit(solution)/shard_map/psum | solution.py:52
  507.6 12.3 %psum.37 = f32[]{:T(128)} all-reduce(f32[]{:T(128)} %psum.36), channel_id=1, replica_groups=mesh['dp_0'=4,'dp_1'=4,'dp_2'=4,'mp_0'=2,'mp_1'=2] {'dp_2'}, use_global_device_ids=true, to_apply=%region_9.10 | all-reduce | flops 1 | bytes 8 | tf_op jit(solution)/shard_map/psum | solution.py:52
  519.9 4.4 psum.38
  524.3 7.3 %psum.39 = f32[]{:T(128)} all-reduce(f32[]{:T(128)} %psum.38), channel_id=1, replica_groups=mesh['dp_0'=4,'dp_1'=4,'dp_2'=4,'mp_0'=2,'mp_1'=2] {'mp_1'}, use_global_device_ids=true, to_apply=%region_11.12 | all-reduce | flops 1 | bytes 8 | tf_op jit(solution)/shard_map/psum | solution.py:52
  532.3 2.1 convert_reduce_fusion.3
  537.1 2.8 convert_reduce_fusion
  (152 shorter events, 20.6 us)
Async XLA Ops:
  7.2 18.6 %copy-start.16 = (f32[8,512]{1,0:T(8,128)S(1)}, f32[8,512]{1,0:T(8,128)}, u32[]{:S(2)}) copy-start(f32[8,512]{1,0:T(8,128)} %param.9) | copy-start | bytes 49156
  7.2 19.1 %copy-start.28 = (bf16[2,20]{1,0:T(2,128)(2,1)S(1)}, bf16[2,20]{1,0:T(2,128)(2,1)}, u32[]{:S(2)}) copy-start(bf16[2,20]{1,0:T(2,128)(2,1)} %param.12) | copy-start | bytes 244
  7.2 19.2 %copy-start.23 = (bf16[32,20]{0,1:T(8,128)(2,1)S(1)}, bf16[32,20]{0,1:T(8,128)(2,1)}, u32[]{:S(2)}) copy-start(bf16[32,20]{0,1:T(8,128)(2,1)} %param.11) | copy-start | bytes 3844
  7.2 206.5 %all-gather.4.cloned.1.call-start = ((), (), s32[]{:S(2)}) async-start(), calls=%async_computation.7 | async-start | bytes 3993600 | tf_op jit(solution)/shard_map/all_gather | solution.py:38
  10.6 202.6 %all-to-all-start = ((bf16[64,320,20]{1,2,0:T(8,128)(2,1)}), bf16[64,320,20]{1,2,0:T(8,128)(2,1)S(1)}, u32[]{:S(2)}, u32[]{:S(2)}) async-start(bf16[64,320,20]{1,2,0:T(8,128)(2,1)} %stack.2), calls=%async_computation | async-start | bytes 2359296 | tf_op jit(solution)/shard_map/all_to_all | solution.py:237
  26.3 186.8 %copy-start.12 = (bf16[128,32]{1,0:T(8,128)(2,1)}, bf16[128,32]{1,0:T(8,128)(2,1)S(1)}, u32[]{:S(2)}) copy-start(bf16[128,32]{1,0:T(8,128)(2,1)S(1)} %convert_element_type.104) | copy-start | bytes 24580
  213.0 7.1 %copy-start.24 = (f32[128]{0:T(128)}, f32[128]{0:T(128)S(1)}, u32[]{:S(2)}) copy-start(f32[128]{0:T(128)S(1)} %add_rsqrt_fusion.1) | copy-start | bytes 1540
  213.2 11.0 %copy-start.2 = (bf16[128,1280]{1,0:T(8,128)(2,1)}, bf16[128,1280]{1,0:T(8,128)(2,1)S(1)}, u32[]{:S(2)}) copy-start(bf16[128,1280]{1,0:T(8,128)(2,1)S(1)} %multiply_convert_fusion.1) | copy-start | bytes 983044
  213.6 13.7 %copy-start = (bf16[320,1280]{0,1:T(8,128)(2,1)}, bf16[320,1280]{0,1:T(8,128)(2,1)S(1)}, u32[]{:S(2)}) copy-start(bf16[320,1280]{0,1:T(8,128)(2,1)S(1)} %reshape.143) | copy-start | bytes 2457604
  226.1 0.8 copy-start.10
  226.4 3.1 copy-start.17
  226.7 2.9 copy-start.19
  226.9 2.6 copy-start.29
  227.4 2.2 copy-start.7
  229.5 32.1 %copy-start.26 = (f32[8,128]{1,0:T(8,128)S(1)}, f32[8,128]{1,0:T(8,128)}, u32[]{:S(2)}) copy-start(f32[8,128]{1,0:T(8,128)} %param.10) | copy-start | bytes 12292
  229.5 61.0 %all-to-all-start.1 = ((f32[4,128,1280]{2,1,0:T(8,128)}), f32[4,128,1280]{2,1,0:T(8,128)S(1)}, u32[]{:S(2)}, u32[]{:S(2)}) async-start(f32[4,128,1280]{2,1,0:T(8,128)} %broadcast_in_dim.61), calls=%async_computation.1 | async-start | bytes 5242880 | tf_op jit(solution)/shard_map/all_to_all | solution.py:43
  264.1 28.7 %copy-start.14 = (f32[128,320]{0,1:T(8,128)S(1)}, f32[128,320]{0,1:T(8,128)}, u32[]{:S(2)}) copy-start(f32[128,320]{0,1:T(8,128)} %sub.62) | copy-start | bytes 491524
  264.1 28.7 %copy-start.22 = (f32[320]{0:T(512)S(1)}, f32[320]{0:T(512)}, u32[]{:S(2)}) copy-start(f32[320]{0:T(512)} %mul.236) | copy-start | bytes 3844
  264.1 28.7 %copy-start.27 = (pred[320]{0:T(512)(128)(4,1)S(1)}, pred[320]{0:T(512)(128)(4,1)}, u32[]{:S(2)}) copy-start(pred[320]{0:T(512)(128)(4,1)} %broadcast_in_dim.30) | copy-start | bytes 964
  295.8 3.2 copy-start.15
  295.8 8.5 %copy-start.30 = (f32[8,4,16,16]{2,3,1,0:T(8,128)S(1)}, f32[8,4,16,16]{2,3,1,0:T(8,128)}, u32[]{:S(2)}) copy-start(f32[8,4,16,16]{2,3,1,0:T(8,128)} %copy-done.29) | copy-start | bytes 98308
  299.0 21.6 %all-to-all-start.2 = ((bf16[4,128,1280]{2,1,0:T(8,128)(2,1)}), bf16[4,128,1280]{2,1,0:T(8,128)(2,1)}, u32[]{:S(2)}, u32[]{:S(2)}) async-start(bf16[4,128,1280]{2,1,0:T(8,128)(2,1)} %broadcast_in_dim.62), calls=%async_computation.2 | async-start | bytes 2621440 | tf_op jit(solution)/shard_map/all_to_all | solution.py:43
  304.2 18.4 %copy-start.1 = (bf16[320,1280]{0,1:T(8,128)(2,1)S(1)}, bf16[320,1280]{0,1:T(8,128)(2,1)}, u32[]{:S(2)}) copy-start(bf16[320,1280]{0,1:T(8,128)(2,1)} %copy-done) | copy-start | bytes 2457604
  305.0 18.4 %copy-start.11 = (bf16[8,16,4,80]{3,2,1,0:T(4,128)(2,1)S(1)}, bf16[8,16,4,80]{3,2,1,0:T(4,128)(2,1)}, u32[]{:S(2)}) copy-start(bf16[8,16,4,80]{3,2,1,0:T(4,128)(2,1)} %copy-done.10) | copy-start | bytes 245764
  322.2 1.5 copy-start.18
  322.2 2.7 copy-start.20
  327.7 5.6 %copy-start.8 = (bf16[128,320]{1,0:T(8,128)(2,1)}, bf16[128,320]{1,0:T(8,128)(2,1)S(1)}, u32[]{:S(2)}) copy-start(bf16[128,320]{1,0:T(8,128)(2,1)S(1)} %reshape.145) | copy-start | bytes 245764
  334.4 20.8 %all-to-all-start.3 = ((bf16[4,128,1280]{2,1,0:T(8,128)(2,1)}), bf16[4,128,1280]{2,1,0:T(8,128)(2,1)S(1)}, u32[]{:S(2)}, u32[]{:S(2)}) async-start(bf16[4,128,1280]{2,1,0:T(8,128)(2,1)} %broadcast_in_dim.63), calls=%async_computation.3 | async-start | bytes 2621440 | tf_op jit(solution)/shard_map/all_to_all | solution.py:43
  341.2 6.9 %copy-start.3 = (bf16[128,1280]{1,0:T(8,128)(2,1)S(1)}, bf16[128,1280]{1,0:T(8,128)(2,1)}, u32[]{:S(2)}) copy-start(bf16[128,1280]{1,0:T(8,128)(2,1)} %copy-done.2) | copy-start | bytes 983044
  345.8 14.8 %copy-start.9 = (bf16[128,320]{1,0:T(8,128)(2,1)S(1)}, bf16[128,320]{1,0:T(8,128)(2,1)}, u32[]{:S(2)}) copy-start(bf16[128,320]{1,0:T(8,128)(2,1)} %copy-done.8) | copy-start | bytes 245764
  349.3 12.8 %copy-start.25 = (f32[128]{0:T(128)S(1)}, f32[128]{0:T(128)}, u32[]{:S(2)}) copy-start(f32[128]{0:T(128)} %copy-done.24) | copy-start | bytes 1540
  355.2 37.8 %all-to-all-start.6 = ((bf16[64,320,20]{1,2,0:T(8,128)(2,1)}), bf16[64,320,20]{1,2,0:T(8,128)(2,1)}, u32[]{:S(2)}, u32[]{:S(2)}) async-start(bf16[64,320,20]{1,2,0:T(8,128)(2,1)} %bitcast.56), calls=%async_computation.6 | async-start | bytes 2359296 | tf_op jit(solution)/shard_map/all_to_all | solution.py:67
  362.0 1.1 copy-start.13
  362.5 37.5 %copy-start.4 = (bf16[1280,320]{0,1:T(8,128)(2,1)S(1)}, bf16[1280,320]{0,1:T(8,128)(2,1)}, u32[]{:S(2)}) copy-start(bf16[1280,320]{0,1:T(8,128)(2,1)} %convolution_convert_fusion.2) | copy-start | bytes 2457604
  362.8 37.3 %copy-start.5 = (bf16[1280,320]{0,1:T(8,128)(2,1)S(1)}, bf16[1280,320]{0,1:T(8,128)(2,1)}, u32[]{:S(2)}) copy-start(bf16[1280,320]{0,1:T(8,128)(2,1)} %convolution_convert_fusion.3) | copy-start | bytes 2457604
  362.8 37.3 %copy-start.6 = (bf16[1280,320]{0,1:T(8,128)(2,1)S(1)}, bf16[1280,320]{0,1:T(8,128)(2,1)}, u32[]{:S(2)}) copy-start(bf16[1280,320]{0,1:T(8,128)(2,1)} %convolution_convert_fusion.4) | copy-start | bytes 2457604
  392.9 19.6 %all-to-all-start.4 = ((f32[64,1,680]{2,1,0:T(1,128)}), f32[64,1,680]{2,1,0:T(1,128)S(1)}, u32[]{:S(2)}, u32[]{:S(2)}) async-start(f32[64,1,680]{2,1,0:T(1,128)} %reshape.158), calls=%async_computation.4 | async-start | bytes 393216 | tf_op jit(solution)/shard_map/all_to_all | solution.py:82
  412.5 124.6 %all-to-all-start.5 = ((bf16[64,20,1280]{2,1,0:T(8,128)(2,1)}), bf16[64,20,1280]{2,1,0:T(8,128)(2,1)}, u32[]{:S(2)}, u32[]{:S(2)}) async-start(bf16[64,20,1280]{2,1,0:T(8,128)(2,1)} %reshape.148), calls=%async_computation.5 | async-start | bytes 7864320 | tf_op jit(solution)/shard_map/all_to_all | solution.py:67
  536.4 4.2 copy-start.21
Sparse Core Ops, SparseCore 0:
  11.2 96.7 all-gather.3
